TPU v7x, 32 devices: a whole 2x2x4 slice. The times are simulated.
32 devices in a mesh: layer: 2 (over core), row: 4 (over y, x), col: 4 (over z).
Axes of the slice: x: 2, y: 2, z: 4, core: 2. Of those that a mesh axis runs over, the one named last changes fastest.
Arguments:
- root_rhs: float32 [32, 8, 1024], P(None, None, 'row'), may hold values from -6 to 6
- child_rhs: float32 [2, 32, 8, 1024], P('layer', None, None, 'row'), may hold values from -6 to 6
- root_factor: float32 [8, 8, 1024, 1024], P(None, None, 'row', 'col'), may hold values from -0.0625 to 0.0625
- child_factor: float32 [2, 8, 8, 1024, 1024], P('layer', None, None, 'row', 'col'), may hold values from -0.0625 to 0.0625
- coupling: float32 [2, 8, 8, 1024, 1024], P('layer', None, None, 'row', 'col'), may hold values from -0.0234375 to 0.0234375
- root_inverse: float32 [8, 1024, 1024], P(None, 'col', 'row'), as said below
- child_inverse: float32 [2, 8, 1024, 1024], P('layer', None, 'col', 'row'), as said below
Outputs:
- root_solution: float32 [32, 8, 1024], P(None, None, 'row')
- child_solution: float32 [2, 32, 8, 1024], P('layer', None, None, 'row')
Inputs may be any that keep to these rules, and one draw needn't show every extreme that they name: Each block of root_inverse is lower triangular. Each block of child_inverse is lower triangular.
All inputs are finite; a program needn't handle non-finite values.
Results may differ from a plain program's by a relative error of at most 0.00015.
Values sent between devices are 32-bit elements; how exact they have to be, the bound alone decides.
No kernel may reach another device: no remote copies, remote signals or barrier semaphores. Data moves between devices by JAX's collectives and lax.ppermute only.
A program may use at most 128 MiB of HBM per device.

v0:
```python
import jax
import jax.numpy as jnp
from jax import lax
from jax.sharding import PartitionSpec as P

precise = lax.Precision.HIGHEST


def pick(stack, index, axis):
    return lax.dynamic_index_in_dim(stack, index, axis, keepdims=False)


def forward(factor, inverse, right, extra, first_col):
    blocks = factor.shape[0]
    columns = right.shape[0]
    col_width = factor.shape[3]
    right_rows = jnp.transpose(right, (1, 0, 2))
    solved = jnp.zeros((blocks, columns, col_width), jnp.float32)

    def forward_step(target, solved):
        row_tiles = pick(factor, target, 0)
        partial_value = jnp.where(first_col, pick(right_rows, target, 0), 0.0) - pick(
            extra, target, 0
        )
        partial_value = partial_value - jnp.einsum(
            "jna,jba->nb", solved, row_tiles, precision=precise
        )
        residual = lax.psum(partial_value, "col")
        share = jnp.einsum("nb,ab->na", residual, pick(inverse, target, 0), precision=precise)
        solved_block = lax.psum(share, "row")
        return lax.dynamic_update_index_in_dim(solved, solved_block, target, 0)

    return lax.fori_loop(0, blocks, forward_step, solved)


def backward(factor, inverse, values, lowered, first_row):
    blocks = factor.shape[0]
    columns = values.shape[1]
    row_width = factor.shape[2]
    solved = jnp.zeros((blocks, columns, row_width), jnp.float32)

    def backward_step(step_at, solved):
        target = blocks - 1 - step_at
        column_tiles = pick(factor, target, 1)
        partial_value = jnp.where(first_row, pick(values, target, 0), 0.0) - pick(
            lowered, target, 0
        )
        partial_value = partial_value - jnp.einsum(
            "inb,iba->na", solved, column_tiles, precision=precise
        )
        pending = lax.psum(partial_value, "row")
        share = jnp.einsum("na,ab->nb", pending, pick(inverse, target, 0), precision=precise)
        solved_block = lax.psum(share, "col")
        return lax.dynamic_update_index_in_dim(solved, solved_block, target, 0)

    return lax.fori_loop(0, blocks, backward_step, solved)


def local(root_rhs, child_rhs, root_factor, child_factor, coupling, root_inverse, child_inverse):
    first_row = lax.axis_index("row") == 0
    first_col = lax.axis_index("col") == 0
    columns = root_rhs.shape[0]
    child_blocks = child_factor[0]
    child_inverses = child_inverse[0]
    couple_blocks = coupling[0]
    child_count = child_blocks.shape[0]
    root_count = root_factor.shape[0]
    row_width = root_factor.shape[2]
    col_width = root_factor.shape[3]
    child_down, root_down = (child_inverses, root_inverse)
    child_up, root_up = (child_inverses, root_inverse)
    child_start = jnp.zeros((child_count, columns, row_width), jnp.float32)
    child_forward = forward(child_blocks, child_down, child_rhs[0], child_start, first_col)
    lifted = jnp.einsum("jna,kjba->knb", child_forward, couple_blocks, precision=precise)
    lifted = lax.psum_scatter(lifted, "layer", scatter_dimension=1, tiled=True)
    half_cols = lifted.shape[1]
    layer_index = lax.axis_index("layer")
    right_half = lax.dynamic_slice_in_dim(root_rhs, layer_index * half_cols, half_cols, 0)
    root_forward = forward(root_factor, root_down, right_half, lifted, first_col)
    empty = jnp.zeros((root_count, half_cols, col_width), jnp.float32)
    root_half = backward(root_factor, root_up, root_forward, empty, first_row)
    root_solved = lax.all_gather(root_half, "layer", axis=1, tiled=True)
    lowered = jnp.einsum("inb,ikba->kna", root_solved, couple_blocks, precision=precise)
    child_solved = backward(child_blocks, child_up, child_forward, lowered, first_row)
    root_solution = jnp.transpose(root_solved, (1, 0, 2))
    child_solution = jnp.transpose(child_solved, (1, 0, 2))[None]
    return (root_solution, child_solution)


def solution(mesh):
    in_specs = (
        P(None, None, "row"),
        P("layer", None, None, "row"),
        P(None, None, "row", "col"),
        P("layer", None, None, "row", "col"),
        P("layer", None, None, "row", "col"),
        P(None, "col", "row"),
        P("layer", None, "col", "row"),
    )
    out_specs = (P(None, None, "row"), P("layer", None, None, "row"))
    return jax.shard_map(local, mesh=mesh, in_specs=in_specs, out_specs=out_specs, check_vma=False)
```

profile of v0, /device:TPU:0, one launch (start us, length us, event | category | flops | bytes accessed | tf_op | source)
XLA Modules:
  0.0 1199.0 jit_solution(10742382642102309621)
XLA Ops:
  8.3 295.6 %while.56 = (s32[]{:T(128)}, f32[8,32,256]{2,1,0:T(8,128)S(1)}, pred[]{:T(512)}, f32[8,32,256]{2,1,0:T(8,128)S(1)}, f32[8,8,256,256]{3,2,1,0:T(8,128)}, /*index=5*/f32[8,256,256]{2,1,0:T(8,128)}, s32[]{:T(128)}) while((s32[]{:T(128)}, f32[8,32,256]{2,1,0:T(8,128)S(1)}, pred[]{:T(512)}, f32[8,32,256]{2,1,0:T(8,128)S(1)}, ...), condition=%wide.region_3.4_spmd, body=%wide.region_0.3_spmd.sunk | while | flops 226525184 | bytes 2950749 | solution.py:33
  11.8 20.9 %psum.108 = f32[32,256]{1,0:T(8,128)S(1)} all-reduce(f32[32,256]{1,0:T(8,128)S(1)} %fusion.96), channel_id=1, replica_groups=mesh['layer'=2,'row'=4,'col'=4] {'col'}, use_global_device_ids=true, to_apply=%region_1.1 | all-reduce | flops 8192 | bytes 65536 | tf_op jit(solution)/shard_map/while/body/eval_jaxpr/psum | solution.py:28
  34.0 16.3 %psum.109 = f32[1,32,256]{2,1,0:T(8,128)S(1)} all-reduce(f32[1,32,256]{2,1,0:T(8,128)S(1)} %convolution_bitcast_fusion.8), channel_id=1, replica_groups=mesh['layer'=2,'row'=4,'col'=4] {'row'}, use_global_device_ids=true, to_apply=%region_2.2 | all-reduce | flops 8192 | bytes 65536 | tf_op jit(solution)/shard_map/while/body/eval_jaxpr/psum | solution.py:30
  53.8 15.8 %psum.108 = f32[32,256]{1,0:T(8,128)S(1)} all-reduce(f32[32,256]{1,0:T(8,128)S(1)} %fusion.96), channel_id=1, replica_groups=mesh['layer'=2,'row'=4,'col'=4] {'col'}, use_global_device_ids=true, to_apply=%region_1.1 | all-reduce | flops 8192 | bytes 65536 | tf_op jit(solution)/shard_map/while/body/eval_jaxpr/psum | solution.py:28
  88.6 17.5 %psum.108 = f32[32,256]{1,0:T(8,128)S(1)} all-reduce(f32[32,256]{1,0:T(8,128)S(1)} %fusion.96), channel_id=1, replica_groups=mesh['layer'=2,'row'=4,'col'=4] {'col'}, use_global_device_ids=true, to_apply=%region_1.1 | all-reduce | flops 8192 | bytes 65536 | tf_op jit(solution)/shard_map/while/body/eval_jaxpr/psum | solution.py:28
  126.5 15.8 %psum.108 = f32[32,256]{1,0:T(8,128)S(1)} all-reduce(f32[32,256]{1,0:T(8,128)S(1)} %fusion.96), channel_id=1, replica_groups=mesh['layer'=2,'row'=4,'col'=4] {'col'}, use_global_device_ids=true, to_apply=%region_1.1 | all-reduce | flops 8192 | bytes 65536 | tf_op jit(solution)/shard_map/while/body/eval_jaxpr/psum | solution.py:28
  161.3 17.5 %psum.108 = f32[32,256]{1,0:T(8,128)S(1)} all-reduce(f32[32,256]{1,0:T(8,128)S(1)} %fusion.96), channel_id=1, replica_groups=mesh['layer'=2,'row'=4,'col'=4] {'col'}, use_global_device_ids=true, to_apply=%region_1.1 | all-reduce | flops 8192 | bytes 65536 | tf_op jit(solution)/shard_map/while/body/eval_jaxpr/psum | solution.py:28
  180.1 16.3 %psum.109 = f32[1,32,256]{2,1,0:T(8,128)S(1)} all-reduce(f32[1,32,256]{2,1,0:T(8,128)S(1)} %convolution_bitcast_fusion.8), channel_id=1, replica_groups=mesh['layer'=2,'row'=4,'col'=4] {'row'}, use_global_device_ids=true, to_apply=%region_2.2 | all-reduce | flops 8192 | bytes 65536 | tf_op jit(solution)/shard_map/while/body/eval_jaxpr/psum | solution.py:30
  199.9 15.8 %psum.108 = f32[32,256]{1,0:T(8,128)S(1)} all-reduce(f32[32,256]{1,0:T(8,128)S(1)} %fusion.96), channel_id=1, replica_groups=mesh['layer'=2,'row'=4,'col'=4] {'col'}, use_global_device_ids=true, to_apply=%region_1.1 | all-reduce | flops 8192 | bytes 65536 | tf_op jit(solution)/shard_map/while/body/eval_jaxpr/psum | solution.py:28
  234.8 17.4 %psum.108 = f32[32,256]{1,0:T(8,128)S(1)} all-reduce(f32[32,256]{1,0:T(8,128)S(1)} %fusion.96), channel_id=1, replica_groups=mesh['layer'=2,'row'=4,'col'=4] {'col'}, use_global_device_ids=true, to_apply=%region_1.1 | all-reduce | flops 8192 | bytes 65536 | tf_op jit(solution)/shard_map/while/body/eval_jaxpr/psum | solution.py:28
  272.6 15.8 %psum.108 = f32[32,256]{1,0:T(8,128)S(1)} all-reduce(f32[32,256]{1,0:T(8,128)S(1)} %fusion.96), channel_id=1, replica_groups=mesh['layer'=2,'row'=4,'col'=4] {'col'}, use_global_device_ids=true, to_apply=%region_1.1 | all-reduce | flops 8192 | bytes 65536 | tf_op jit(solution)/shard_map/while/body/eval_jaxpr/psum | solution.py:28
  303.9 19.2 %fusion.56 = f32[8,32,256]{2,1,0:T(8,128)} fusion(f32[1,8,8,256,256]{4,3,2,1,0:T(8,128)} %param.19, f32[8,32,256]{2,1,0:T(8,128)S(1)} %get-tuple-element.861), kind=kOutput, calls=%fused_computation.48 | convolution fusion | flops 1610612736 | bytes 17301504 | tf_op jit(solution)/shard_map/jna,kjba->knb/dot_general | solution.py:74
  330.4 284.1 %while.57 = (s32[]{:T(128)}, f32[8,16,256]{2,1,0:T(8,128)S(1)}, pred[]{:T(512)}, f32[8,16,256]{2,1,0:T(8,128)S(1)}, f32[8,16,256]{2,1,0:T(8,128)}, /*index=5*/f3...) while((s32[]{:T(128)}, f32[8,16,256]{2,1,0:T(8,128)S(1)}, pred[]{:T(512)}, ...), condition=%wide.region_8.9_spmd, body=%wide.region_5.8_spmd.sunk | while | flops 113266688 | bytes 2672229 | solution.py:33
  333.7 18.9 %psum.110 = f32[16,256]{1,0:T(8,128)S(1)} all-reduce(f32[16,256]{1,0:T(8,128)S(1)} %fusion.101), channel_id=1, replica_groups=mesh['layer'=2,'row'=4,'col'=4] {'col'}, use_global_device_ids=true, to_apply=%region_6.6 | all-reduce | flops 4096 | bytes 32768 | tf_op jit(solution)/shard_map/while/body/eval_jaxpr/psum | solution.py:28
  353.9 16.1 %psum.111 = f32[1,16,256]{2,1,0:T(8,128)S(1)} all-reduce(f32[1,16,256]{2,1,0:T(8,128)S(1)} %convolution_bitcast_fusion.9), channel_id=1, replica_groups=mesh['layer'=2,'row'=4,'col'=4] {'row'}, use_global_device_ids=true, to_apply=%region_7.7 | all-reduce | flops 4096 | bytes 32768 | tf_op jit(solution)/shard_map/while/body/eval_jaxpr/psum | solution.py:30
  407.2 16.3 %psum.110 = f32[16,256]{1,0:T(8,128)S(1)} all-reduce(f32[16,256]{1,0:T(8,128)S(1)} %fusion.101), channel_id=1, replica_groups=mesh['layer'=2,'row'=4,'col'=4] {'col'}, use_global_device_ids=true, to_apply=%region_6.6 | all-reduce | flops 4096 | bytes 32768 | tf_op jit(solution)/shard_map/while/body/eval_jaxpr/psum | solution.py:28
  477.4 16.3 %psum.110 = f32[16,256]{1,0:T(8,128)S(1)} all-reduce(f32[16,256]{1,0:T(8,128)S(1)} %fusion.101), channel_id=1, replica_groups=mesh['layer'=2,'row'=4,'col'=4] {'col'}, use_global_device_ids=true, to_apply=%region_6.6 | all-reduce | flops 4096 | bytes 32768 | tf_op jit(solution)/shard_map/while/body/eval_jaxpr/psum | solution.py:28
  547.6 16.3 %psum.110 = f32[16,256]{1,0:T(8,128)S(1)} all-reduce(f32[16,256]{1,0:T(8,128)S(1)} %fusion.101), channel_id=1, replica_groups=mesh['layer'=2,'row'=4,'col'=4] {'col'}, use_global_device_ids=true, to_apply=%region_6.6 | all-reduce | flops 4096 | bytes 32768 | tf_op jit(solution)/shard_map/while/body/eval_jaxpr/psum | solution.py:28
  614.5 274.9 %while.58 = (s32[]{:T(128)}, f32[8,16,256]{2,1,0:T(8,128)S(1)}, pred[]{:T(512)}, f32[8,16,256]{2,1,0:T(8,128)S(1)}, f32[8,8,256,256]{3,2,1,0:T(8,128)}, /*index=...) while((s32[]{:T(128)}, f32[8,16,256]{2,1,0:T(8,128)S(1)}, pred[]{:T(512)}, ...), condition=%wide.region_12.13_spmd, body=%wide.region_9.12_spmd.sunk | while | flops 113262600 | bytes 2655907 | solution.py:56
  633.8 16.3 %psum.113 = f32[1,16,256]{2,1,0:T(8,128)S(1)} all-reduce(f32[1,16,256]{2,1,0:T(8,128)S(1)} %convolution_bitcast_fusion.10), channel_id=1, replica_groups=mesh['layer'=2,'row'=4,'col'=4] {'col'}, use_global_device_ids=true, to_apply=%region_11.11 | all-reduce | flops 4096 | bytes 32768 | tf_op jit(solution)/shard_map/while/body/eval_jaxpr/psum | solution.py:53
  702.5 16.2 %psum.113 = f32[1,16,256]{2,1,0:T(8,128)S(1)} all-reduce(f32[1,16,256]{2,1,0:T(8,128)S(1)} %convolution_bitcast_fusion.10), channel_id=1, replica_groups=mesh['layer'=2,'row'=4,'col'=4] {'col'}, use_global_device_ids=true, to_apply=%region_11.11 | all-reduce | flops 4096 | bytes 32768 | tf_op jit(solution)/shard_map/while/body/eval_jaxpr/psum | solution.py:53
  771.2 16.3 %psum.113 = f32[1,16,256]{2,1,0:T(8,128)S(1)} all-reduce(f32[1,16,256]{2,1,0:T(8,128)S(1)} %convolution_bitcast_fusion.10), channel_id=1, replica_groups=mesh['layer'=2,'row'=4,'col'=4] {'col'}, use_global_device_ids=true, to_apply=%region_11.11 | all-reduce | flops 4096 | bytes 32768 | tf_op jit(solution)/shard_map/while/body/eval_jaxpr/psum | solution.py:53
  839.9 16.3 %psum.113 = f32[1,16,256]{2,1,0:T(8,128)S(1)} all-reduce(f32[1,16,256]{2,1,0:T(8,128)S(1)} %convolution_bitcast_fusion.10), channel_id=1, replica_groups=mesh['layer'=2,'row'=4,'col'=4] {'col'}, use_global_device_ids=true, to_apply=%region_11.11 | all-reduce | flops 4096 | bytes 32768 | tf_op jit(solution)/shard_map/while/body/eval_jaxpr/psum | solution.py:53
  905.6 285.7 %while.59 = (s32[]{:T(128)}, f32[8,32,256]{2,1,0:T(8,128)S(1)}, pred[]{:T(512)}, f32[8,32,256]{2,1,0:T(8,128)S(1)}, f32[8,32,256]{2,1,0:T(8,128)S(1)}, /*index=5...) while((s32[]{:T(128)}, f32[8,32,256]{2,1,0:T(8,128)S(1)}, ...), condition=%wide.region_16.17_spmd, body=%wide.region_13.16_spmd.sunk | while | flops 226533376 | bytes 2983595 | solution.py:56
  925.2 16.6 %psum.115 = f32[1,32,256]{2,1,0:T(8,128)S(1)} all-reduce(f32[1,32,256]{2,1,0:T(8,128)S(1)} %convolution_bitcast_fusion.11), channel_id=1, replica_groups=mesh['layer'=2,'row'=4,'col'=4] {'col'}, use_global_device_ids=true, to_apply=%region_15.15 | all-reduce | flops 8192 | bytes 65536 | tf_op jit(solution)/shard_map/while/body/eval_jaxpr/psum | solution.py:53
  960.0 16.7 %psum.115 = f32[1,32,256]{2,1,0:T(8,128)S(1)} all-reduce(f32[1,32,256]{2,1,0:T(8,128)S(1)} %convolution_bitcast_fusion.11), channel_id=1, replica_groups=mesh['layer'=2,'row'=4,'col'=4] {'col'}, use_global_device_ids=true, to_apply=%region_15.15 | all-reduce | flops 8192 | bytes 65536 | tf_op jit(solution)/shard_map/while/body/eval_jaxpr/psum | solution.py:53
  996.2 16.6 %psum.115 = f32[1,32,256]{2,1,0:T(8,128)S(1)} all-reduce(f32[1,32,256]{2,1,0:T(8,128)S(1)} %convolution_bitcast_fusion.11), channel_id=1, replica_groups=mesh['layer'=2,'row'=4,'col'=4] {'col'}, use_global_device_ids=true, to_apply=%region_15.15 | all-reduce | flops 8192 | bytes 65536 | tf_op jit(solution)/shard_map/while/body/eval_jaxpr/psum | solution.py:53
  1031.6 16.9 %psum.115 = f32[1,32,256]{2,1,0:T(8,128)S(1)} all-reduce(f32[1,32,256]{2,1,0:T(8,128)S(1)} %convolution_bitcast_fusion.11), channel_id=1, replica_groups=mesh['layer'=2,'row'=4,'col'=4] {'col'}, use_global_device_ids=true, to_apply=%region_15.15 | all-reduce | flops 8192 | bytes 65536 | tf_op jit(solution)/shard_map/while/body/eval_jaxpr/psum | solution.py:53
  1068.0 16.7 %psum.115 = f32[1,32,256]{2,1,0:T(8,128)S(1)} all-reduce(f32[1,32,256]{2,1,0:T(8,128)S(1)} %convolution_bitcast_fusion.11), channel_id=1, replica_groups=mesh['layer'=2,'row'=4,'col'=4] {'col'}, use_global_device_ids=true, to_apply=%region_15.15 | all-reduce | flops 8192 | bytes 65536 | tf_op jit(solution)/shard_map/while/body/eval_jaxpr/psum | solution.py:53
  1103.0 16.7 %psum.115 = f32[1,32,256]{2,1,0:T(8,128)S(1)} all-reduce(f32[1,32,256]{2,1,0:T(8,128)S(1)} %convolution_bitcast_fusion.11), channel_id=1, replica_groups=mesh['layer'=2,'row'=4,'col'=4] {'col'}, use_global_device_ids=true, to_apply=%region_15.15 | all-reduce | flops 8192 | bytes 65536 | tf_op jit(solution)/shard_map/while/body/eval_jaxpr/psum | solution.py:53
  1139.1 16.6 %psum.115 = f32[1,32,256]{2,1,0:T(8,128)S(1)} all-reduce(f32[1,32,256]{2,1,0:T(8,128)S(1)} %convolution_bitcast_fusion.11), channel_id=1, replica_groups=mesh['layer'=2,'row'=4,'col'=4] {'col'}, use_global_device_ids=true, to_apply=%region_15.15 | all-reduce | flops 8192 | bytes 65536 | tf_op jit(solution)/shard_map/while/body/eval_jaxpr/psum | solution.py:53
  1174.3 16.9 %psum.115 = f32[1,32,256]{2,1,0:T(8,128)S(1)} all-reduce(f32[1,32,256]{2,1,0:T(8,128)S(1)} %convolution_bitcast_fusion.11), channel_id=1, replica_groups=mesh['layer'=2,'row'=4,'col'=4] {'col'}, use_global_device_ids=true, to_apply=%region_15.15 | all-reduce | flops 8192 | bytes 65536 | tf_op jit(solution)/shard_map/while/body/eval_jaxpr/psum | solution.py:53
  (149 shorter events, 712.7 us)
Async XLA Ops:
  7.2 316.0 %copy-start = (f32[32,8,256]{2,1,0:T(8,128)S(1)}, f32[32,8,256]{2,1,0:T(8,128)}, u32[]{:S(2)}) copy-start(f32[32,8,256]{2,1,0:T(8,128)} %param.15) | copy-start | bytes 786436
  7.2 323.2 %reduce-scatter.2.cloned.1.call-start = ((), (), s32[]{:S(2)}) async-start(), calls=%async_computation.1 | async-start | bytes 393216 | tf_op jit(solution)/shard_map/reduce_scatter | solution.py:75
Sparse Core Ops, SparseCore 0:
  323.2 7.0 reduce-scatter.1
where the time goes:
time: 1200 us
  blocking collectives  1000 us (83%)
  matrix products  169 us (14%)
  between operations  14.1 us (1%)
    psum x16, blocking collectives, forward_step(): residual = lax.psum(partial_value, 'col')  266 us
    psum x16, blocking collectives, backward_step(): solved_block = lax.psum(share, 'col')  261 us
    psum x16, blocking collectives, forward_step(): solved_block = lax.psum(share, 'row')  238 us
    psum x16, blocking collectives, backward_step(): pending = lax.psum(partial_value, 'row')  236 us
    dot_general x16, matrix products, forward_step(): jnp.einsum('jna,jba->nb', solved, row_tiles, precision=precise)  54.5 us
    dot_general x16, matrix products, backward_step(): jnp.einsum('inb,iba->na', solved, column_tiles, precision=precise)  43.7 us
  transfers between devices with their start and end apart: 1, of which 1 were waited for; matrix products, arithmetic and copies ran while one was open for 0% of the time, Pallas kernels for 0%

commit v1 on v0

--- a/solution.py
+++ b/solution.py
@@ -50,7 +50,7 @@
         )
         pending = lax.psum(partial_value, "row")
         share = jnp.einsum("na,ab->nb", pending, pick(inverse, target, 0), precision=precise)
-        solved_block = lax.psum(share, "col")
+        solved_block = jnp.sum(lax.all_gather(share, "col"), axis=0)
         return lax.dynamic_update_index_in_dim(solved, solved_block, target, 0)
 
     return lax.fori_loop(0, blocks, backward_step, solved)

time: 1200 us -> 1150 us (0.958)
  blocking collectives: 1000 us -> 955 us
    psum x16 -> x0, blocking collectives: 261 us -> none  [backward_step(): solved_block = lax.psum(share, 'col')]
    all_gather x0 -> x16, blocking collectives: none -> 212 us  [backward_step(): solved_block = jnp.sum(lax.all_gather(share, 'col'), axis=0)]
where the time goes in v1:
time: 1150 us
  blocking collectives  955 us (83%)
  matrix products  169 us (15%)
  between operations  14.1 us (1%)
    psum x16, blocking collectives, forward_step(): residual = lax.psum(partial_value, 'col')  266 us
    psum x16, blocking collectives, forward_step(): solved_block = lax.psum(share, 'row')  238 us
    psum x16, blocking collectives, backward_step(): pending = lax.psum(partial_value, 'row')  237 us
    all_gather x16, blocking collectives, backward_step(): solved_block = jnp.sum(lax.all_gather(share, 'col'), axis=0)  212 us
    dot_general x16, matrix products, forward_step(): jnp.einsum('jna,jba->nb', solved, row_tiles, precision=precise)  54.5 us
    dot_general x16, matrix products, backward_step(): jnp.einsum('inb,iba->na', solved, column_tiles, precision=precise)  43.8 us
  transfers between devices with their start and end apart: 1, of which 1 were waited for; matrix products, arithmetic and copies ran while one was open for 0% of the time, Pallas kernels for 0%

profile of v1, /device:TPU:0, one launch (start us, length us, event | category | flops | bytes accessed | tf_op | source)
XLA Modules:
  0.0 1150.8 jit_solution(12990924160389497837)
XLA Ops:
  8.3 295.6 %while.56 = (s32[]{:T(128)}, f32[8,32,256]{2,1,0:T(8,128)S(1)}, pred[]{:T(512)}, f32[8,32,256]{2,1,0:T(8,128)S(1)}, f32[8,8,256,256]{3,2,1,0:T(8,128)}, /*index=5*/f32[8,256,256]{2,1,0:T(8,128)}, s32[]{:T(128)}) while((s32[]{:T(128)}, f32[8,32,256]{2,1,0:T(8,128)S(1)}, pred[]{:T(512)}, f32[8,32,256]{2,1,0:T(8,128)S(1)}, ...), condition=%wide.region_3.4_spmd, body=%wide.region_0.3_spmd.sunk | while | flops 226525184 | bytes 2950749 | solution.py:33
  11.8 20.9 %psum.78 = f32[32,256]{1,0:T(8,128)S(1)} all-reduce(f32[32,256]{1,0:T(8,128)S(1)} %fusion.100), channel_id=1, replica_groups=mesh['layer'=2,'row'=4,'col'=4] {'col'}, use_global_device_ids=true, to_apply=%region_1.1 | all-reduce | flops 8192 | bytes 65536 | tf_op jit(solution)/shard_map/while/body/eval_jaxpr/psum | solution.py:28
  34.0 16.3 %psum.79 = f32[1,32,256]{2,1,0:T(8,128)S(1)} all-reduce(f32[1,32,256]{2,1,0:T(8,128)S(1)} %convolution_bitcast_fusion.4), channel_id=1, replica_groups=mesh['layer'=2,'row'=4,'col'=4] {'row'}, use_global_device_ids=true, to_apply=%region_2.2 | all-reduce | flops 8192 | bytes 65536 | tf_op jit(solution)/shard_map/while/body/eval_jaxpr/psum | solution.py:30
  53.8 15.8 %psum.78 = f32[32,256]{1,0:T(8,128)S(1)} all-reduce(f32[32,256]{1,0:T(8,128)S(1)} %fusion.100), channel_id=1, replica_groups=mesh['layer'=2,'row'=4,'col'=4] {'col'}, use_global_device_ids=true, to_apply=%region_1.1 | all-reduce | flops 8192 | bytes 65536 | tf_op jit(solution)/shard_map/while/body/eval_jaxpr/psum | solution.py:28
  88.6 17.5 %psum.78 = f32[32,256]{1,0:T(8,128)S(1)} all-reduce(f32[32,256]{1,0:T(8,128)S(1)} %fusion.100), channel_id=1, replica_groups=mesh['layer'=2,'row'=4,'col'=4] {'col'}, use_global_device_ids=true, to_apply=%region_1.1 | all-reduce | flops 8192 | bytes 65536 | tf_op jit(solution)/shard_map/while/body/eval_jaxpr/psum | solution.py:28
  107.5 15.6 %psum.79 = f32[1,32,256]{2,1,0:T(8,128)S(1)} all-reduce(f32[1,32,256]{2,1,0:T(8,128)S(1)} %convolution_bitcast_fusion.4), channel_id=1, replica_groups=mesh['layer'=2,'row'=4,'col'=4] {'row'}, use_global_device_ids=true, to_apply=%region_2.2 | all-reduce | flops 8192 | bytes 65536 | tf_op jit(solution)/shard_map/while/body/eval_jaxpr/psum | solution.py:30
  126.5 15.8 %psum.78 = f32[32,256]{1,0:T(8,128)S(1)} all-reduce(f32[32,256]{1,0:T(8,128)S(1)} %fusion.100), channel_id=1, replica_groups=mesh['layer'=2,'row'=4,'col'=4] {'col'}, use_global_device_ids=true, to_apply=%region_1.1 | all-reduce | flops 8192 | bytes 65536 | tf_op jit(solution)/shard_map/while/body/eval_jaxpr/psum | solution.py:28
  161.3 17.5 %psum.78 = f32[32,256]{1,0:T(8,128)S(1)} all-reduce(f32[32,256]{1,0:T(8,128)S(1)} %fusion.100), channel_id=1, replica_groups=mesh['layer'=2,'row'=4,'col'=4] {'col'}, use_global_device_ids=true, to_apply=%region_1.1 | all-reduce | flops 8192 | bytes 65536 | tf_op jit(solution)/shard_map/while/body/eval_jaxpr/psum | solution.py:28
  180.1 16.3 %psum.79 = f32[1,32,256]{2,1,0:T(8,128)S(1)} all-reduce(f32[1,32,256]{2,1,0:T(8,128)S(1)} %convolution_bitcast_fusion.4), channel_id=1, replica_groups=mesh['layer'=2,'row'=4,'col'=4] {'row'}, use_global_device_ids=true, to_apply=%region_2.2 | all-reduce | flops 8192 | bytes 65536 | tf_op jit(solution)/shard_map/while/body/eval_jaxpr/psum | solution.py:30
  199.9 15.8 %psum.78 = f32[32,256]{1,0:T(8,128)S(1)} all-reduce(f32[32,256]{1,0:T(8,128)S(1)} %fusion.100), channel_id=1, replica_groups=mesh['layer'=2,'row'=4,'col'=4] {'col'}, use_global_device_ids=true, to_apply=%region_1.1 | all-reduce | flops 8192 | bytes 65536 | tf_op jit(solution)/shard_map/while/body/eval_jaxpr/psum | solution.py:28
  234.8 17.4 %psum.78 = f32[32,256]{1,0:T(8,128)S(1)} all-reduce(f32[32,256]{1,0:T(8,128)S(1)} %fusion.100), channel_id=1, replica_groups=mesh['layer'=2,'row'=4,'col'=4] {'col'}, use_global_device_ids=true, to_apply=%region_1.1 | all-reduce | flops 8192 | bytes 65536 | tf_op jit(solution)/shard_map/while/body/eval_jaxpr/psum | solution.py:28
  253.5 15.6 %psum.79 = f32[1,32,256]{2,1,0:T(8,128)S(1)} all-reduce(f32[1,32,256]{2,1,0:T(8,128)S(1)} %convolution_bitcast_fusion.4), channel_id=1, replica_groups=mesh['layer'=2,'row'=4,'col'=4] {'row'}, use_global_device_ids=true, to_apply=%region_2.2 | all-reduce | flops 8192 | bytes 65536 | tf_op jit(solution)/shard_map/while/body/eval_jaxpr/psum | solution.py:30
  272.6 15.8 %psum.78 = f32[32,256]{1,0:T(8,128)S(1)} all-reduce(f32[32,256]{1,0:T(8,128)S(1)} %fusion.100), channel_id=1, replica_groups=mesh['layer'=2,'row'=4,'col'=4] {'col'}, use_global_device_ids=true, to_apply=%region_1.1 | all-reduce | flops 8192 | bytes 65536 | tf_op jit(solution)/shard_map/while/body/eval_jaxpr/psum | solution.py:28
  303.9 19.2 %fusion.58 = f32[8,32,256]{2,1,0:T(8,128)} fusion(f32[1,8,8,256,256]{4,3,2,1,0:T(8,128)} %param.19, f32[8,32,256]{2,1,0:T(8,128)S(1)} %get-tuple-element.864), kind=kOutput, calls=%fused_computation.48 | convolution fusion | flops 1610612736 | bytes 17301504 | tf_op jit(solution)/shard_map/jna,kjba->knb/dot_general | solution.py:74
  330.4 284.1 %while.57 = (s32[]{:T(128)}, f32[8,16,256]{2,1,0:T(8,128)S(1)}, pred[]{:T(512)}, f32[8,16,256]{2,1,0:T(8,128)S(1)}, f32[8,16,256]{2,1,0:T(8,128)}, /*index=5*/f3...) while((s32[]{:T(128)}, f32[8,16,256]{2,1,0:T(8,128)S(1)}, pred[]{:T(512)}, ...), condition=%wide.region_8.9_spmd, body=%wide.region_5.8_spmd.sunk | while | flops 113266688 | bytes 2672229 | solution.py:33
  333.7 18.9 %psum.80 = f32[16,256]{1,0:T(8,128)S(1)} all-reduce(f32[16,256]{1,0:T(8,128)S(1)} %fusion.105), channel_id=1, replica_groups=mesh['layer'=2,'row'=4,'col'=4] {'col'}, use_global_device_ids=true, to_apply=%region_6.6 | all-reduce | flops 4096 | bytes 32768 | tf_op jit(solution)/shard_map/while/body/eval_jaxpr/psum | solution.py:28
  353.9 16.1 %psum.81 = f32[1,16,256]{2,1,0:T(8,128)S(1)} all-reduce(f32[1,16,256]{2,1,0:T(8,128)S(1)} %convolution_bitcast_fusion.5), channel_id=1, replica_groups=mesh['layer'=2,'row'=4,'col'=4] {'row'}, use_global_device_ids=true, to_apply=%region_7.7 | all-reduce | flops 4096 | bytes 32768 | tf_op jit(solution)/shard_map/while/body/eval_jaxpr/psum | solution.py:30
  373.3 15.6 %psum.80 = f32[16,256]{1,0:T(8,128)S(1)} all-reduce(f32[16,256]{1,0:T(8,128)S(1)} %fusion.105), channel_id=1, replica_groups=mesh['layer'=2,'row'=4,'col'=4] {'col'}, use_global_device_ids=true, to_apply=%region_6.6 | all-reduce | flops 4096 | bytes 32768 | tf_op jit(solution)/shard_map/while/body/eval_jaxpr/psum | solution.py:28
  407.2 16.3 %psum.80 = f32[16,256]{1,0:T(8,128)S(1)} all-reduce(f32[16,256]{1,0:T(8,128)S(1)} %fusion.105), channel_id=1, replica_groups=mesh['layer'=2,'row'=4,'col'=4] {'col'}, use_global_device_ids=true, to_apply=%region_6.6 | all-reduce | flops 4096 | bytes 32768 | tf_op jit(solution)/shard_map/while/body/eval_jaxpr/psum | solution.py:28
  424.7 15.4 %psum.81 = f32[1,16,256]{2,1,0:T(8,128)S(1)} all-reduce(f32[1,16,256]{2,1,0:T(8,128)S(1)} %convolution_bitcast_fusion.5), channel_id=1, replica_groups=mesh['layer'=2,'row'=4,'col'=4] {'row'}, use_global_device_ids=true, to_apply=%region_7.7 | all-reduce | flops 4096 | bytes 32768 | tf_op jit(solution)/shard_map/while/body/eval_jaxpr/psum | solution.py:30
  443.5 15.6 %psum.80 = f32[16,256]{1,0:T(8,128)S(1)} all-reduce(f32[16,256]{1,0:T(8,128)S(1)} %fusion.105), channel_id=1, replica_groups=mesh['layer'=2,'row'=4,'col'=4] {'col'}, use_global_device_ids=true, to_apply=%region_6.6 | all-reduce | flops 4096 | bytes 32768 | tf_op jit(solution)/shard_map/while/body/eval_jaxpr/psum | solution.py:28
  477.4 16.3 %psum.80 = f32[16,256]{1,0:T(8,128)S(1)} all-reduce(f32[16,256]{1,0:T(8,128)S(1)} %fusion.105), channel_id=1, replica_groups=mesh['layer'=2,'row'=4,'col'=4] {'col'}, use_global_device_ids=true, to_apply=%region_6.6 | all-reduce | flops 4096 | bytes 32768 | tf_op jit(solution)/shard_map/while/body/eval_jaxpr/psum | solution.py:28
  513.7 15.6 %psum.80 = f32[16,256]{1,0:T(8,128)S(1)} all-reduce(f32[16,256]{1,0:T(8,128)S(1)} %fusion.105), channel_id=1, replica_groups=mesh['layer'=2,'row'=4,'col'=4] {'col'}, use_global_device_ids=true, to_apply=%region_6.6 | all-reduce | flops 4096 | bytes 32768 | tf_op jit(solution)/shard_map/while/body/eval_jaxpr/psum | solution.py:28
  547.6 16.3 %psum.80 = f32[16,256]{1,0:T(8,128)S(1)} all-reduce(f32[16,256]{1,0:T(8,128)S(1)} %fusion.105), channel_id=1, replica_groups=mesh['layer'=2,'row'=4,'col'=4] {'col'}, use_global_device_ids=true, to_apply=%region_6.6 | all-reduce | flops 4096 | bytes 32768 | tf_op jit(solution)/shard_map/while/body/eval_jaxpr/psum | solution.py:28
  583.9 15.6 %psum.80 = f32[16,256]{1,0:T(8,128)S(1)} all-reduce(f32[16,256]{1,0:T(8,128)S(1)} %fusion.105), channel_id=1, replica_groups=mesh['layer'=2,'row'=4,'col'=4] {'col'}, use_global_device_ids=true, to_apply=%region_6.6 | all-reduce | flops 4096 | bytes 32768 | tf_op jit(solution)/shard_map/while/body/eval_jaxpr/psum | solution.py:28
  614.5 253.1 %while.58 = (s32[]{:T(128)}, f32[8,16,256]{2,1,0:T(8,128)S(1)}, pred[]{:T(512)}, f32[8,16,256]{2,1,0:T(8,128)S(1)}, f32[8,8,256,256]{3,2,1,0:T(8,128)}, /*index=...) while((s32[]{:T(128)}, f32[8,16,256]{2,1,0:T(8,128)S(1)}, ...), condition=%wide.region_12.13_spmd, body=%wide.region_9.12_spmd.sunk | while | flops 113270792 | bytes 2786991 | solution.py:56
  680.4 15.4 %psum.82 = f32[16,256]{1,0:T(8,128)S(1)} all-reduce(f32[16,256]{1,0:T(8,128)S(1)} %fusion.110), channel_id=1, replica_groups=mesh['layer'=2,'row'=4,'col'=4] {'row'}, use_global_device_ids=true, to_apply=%region_10.10 | all-reduce | flops 4096 | bytes 32768 | tf_op jit(solution)/shard_map/while/body/eval_jaxpr/psum | solution.py:51
  883.8 259.3 %while.59 = (s32[]{:T(128)}, f32[8,32,256]{2,1,0:T(8,128)S(1)}, pred[]{:T(512)}, f32[8,32,256]{2,1,0:T(8,128)S(1)}, f32[8,32,256]{2,1,0:T(8,128)S(1)}, /*index=5...) while((s32[]{:T(128)}, f32[8,32,256]{2,1,0:T(8,128)S(1)}, ...), condition=%wide.region_16.17_spmd, body=%wide.region_13.16_spmd.sunk | while | flops 226549760 | bytes 3245751 | solution.py:56
  886.6 15.6 %psum.83 = f32[32,256]{1,0:T(8,128)S(1)} all-reduce(f32[32,256]{1,0:T(8,128)S(1)} %fusion.116), channel_id=1, replica_groups=mesh['layer'=2,'row'=4,'col'=4] {'row'}, use_global_device_ids=true, to_apply=%region_14.14 | all-reduce | flops 8192 | bytes 65536 | tf_op jit(solution)/shard_map/while/body/eval_jaxpr/psum | solution.py:51
  951.1 15.6 %psum.83 = f32[32,256]{1,0:T(8,128)S(1)} all-reduce(f32[32,256]{1,0:T(8,128)S(1)} %fusion.116), channel_id=1, replica_groups=mesh['layer'=2,'row'=4,'col'=4] {'row'}, use_global_device_ids=true, to_apply=%region_14.14 | all-reduce | flops 8192 | bytes 65536 | tf_op jit(solution)/shard_map/while/body/eval_jaxpr/psum | solution.py:51
  1016.3 15.8 %psum.83 = f32[32,256]{1,0:T(8,128)S(1)} all-reduce(f32[32,256]{1,0:T(8,128)S(1)} %fusion.116), channel_id=1, replica_groups=mesh['layer'=2,'row'=4,'col'=4] {'row'}, use_global_device_ids=true, to_apply=%region_14.14 | all-reduce | flops 8192 | bytes 65536 | tf_op jit(solution)/shard_map/while/body/eval_jaxpr/psum | solution.py:51
  1080.8 15.7 %psum.83 = f32[32,256]{1,0:T(8,128)S(1)} all-reduce(f32[32,256]{1,0:T(8,128)S(1)} %fusion.116), channel_id=1, replica_groups=mesh['layer'=2,'row'=4,'col'=4] {'row'}, use_global_device_ids=true, to_apply=%region_14.14 | all-reduce | flops 8192 | bytes 65536 | tf_op jit(solution)/shard_map/while/body/eval_jaxpr/psum | solution.py:51
  (165 shorter events, 676.1 us)
Async XLA Ops:
  7.2 316.0 %copy-start = (f32[32,8,256]{2,1,0:T(8,128)S(1)}, f32[32,8,256]{2,1,0:T(8,128)}, u32[]{:S(2)}) copy-start(f32[32,8,256]{2,1,0:T(8,128)} %param.15) | copy-start | bytes 786436
  7.2 323.2 %reduce-scatter.2.cloned.1.call-start = ((), (), s32[]{:S(2)}) async-start(), calls=%async_computation.1 | async-start | bytes 393216 | tf_op jit(solution)/shard_map/reduce_scatter | solution.py:75
Sparse Core Ops, SparseCore 0:
  323.2 7.0 reduce-scatter.1
